TPU v7x, 128 devices: a whole 4x4x4 slice. The times are simulated.
128 devices in a mesh: tau: 8 (over x, core), tile: 16 (over z, y).
Axes of the slice: x: 4, y: 4, z: 4, core: 2. Of those that a mesh axis runs over, the one named last changes fastest.
Arguments:
- occupied: bfloat16 [8, 2048, 128, 128], P('tau', 'tile'), may hold values from -6 to 6
- virtual: bfloat16 [8, 2048, 128, 128], P('tau', 'tile'), may hold values from -0.125 to 0.125
- cos_weights: float32 [4, 8], replicated, may hold values from -1 to 1
- pair_occ: int32 [3072, 16], P('tile'), may hold values from 0 to 127
- pair_virt: int32 [3072, 16], P('tile'), may hold values from 0 to 127
- partial_target_tile: int32 [3072], P('tile'), may hold values from 0 to 511, as said below
Outputs:
- spectrum: float32 [4, 512, 128, 128], P(None, 'tile', 'tau')
Inputs may be any that keep to these rules, and one draw needn't show every extreme that they name: `partial_target_tile`: within each aligned block of 192 entries, no owner (values d * 32 to (d + 1) * 32 - 1 for owner d) is named more than 24 times; one owner is named exactly 24 times in every block.
All inputs are finite; a program needn't handle non-finite values.
Results may differ from a plain program's by a relative error of at most 0.0003.
Values sent between devices are 32-bit elements; how exact they have to be, the bound alone decides.
No kernel may reach another device: no remote copies, remote signals or barrier semaphores. Data moves between devices by JAX's collectives and lax.ppermute only.
A program may use at most 192 MiB of HBM per device.

v0:
```python
import math

import jax
import jax.numpy as jnp
from jax import lax
from jax.sharding import PartitionSpec as P

CHI_DEV = 32


def in_one_piece(arrays, axis, split_dim, concat_dim, along):
    columns = [a.reshape(*a.shape[:along], -1) for a in arrays]
    both = jnp.concatenate(columns, axis=along)
    out, at, gathered = (
        lax.all_to_all(both, axis, split_axis=split_dim, concat_axis=concat_dim, tiled=True),
        0,
        [],
    )
    for a, column in zip(arrays, columns):
        piece = out[..., at : at + column.shape[along]]
        gathered.append(piece.reshape(*piece.shape[:along], *a.shape[along:]))
        at += column.shape[along]
    return tuple(gathered)


def block_products(occupied, virtual, occ_index, virt_index, groups):
    tau_count = occupied.shape[0]
    tile_size = occupied.shape[2]
    rows = tile_size // groups
    part_count = occ_index.shape[0]
    terms = occ_index.shape[1]
    group = math.gcd(part_count, 8)
    count = part_count // group
    empty = jnp.zeros((groups, part_count, tau_count, rows, tile_size), jnp.float32)

    def one_block(block, result):
        first = block * group
        occ_rows = lax.dynamic_slice_in_dim(occ_index, first, group, 0)
        virt_rows = lax.dynamic_slice_in_dim(virt_index, first, group, 0)
        left = jnp.take(occupied[0], occ_rows, axis=0)
        right = jnp.take(virtual[0], virt_rows, axis=0)
        left = left.reshape(group, terms, groups, rows, tile_size)
        pieces = [jnp.einsum("bjgrk,bjkc->gbrc", left, right, preferred_element_type=jnp.float32)]
        stacked = jnp.stack(pieces, axis=2)
        return lax.dynamic_update_slice_in_dim(result, stacked, first, 1)

    return lax.fori_loop(0, count, one_block, empty)


def slot_layout(partial_target_tile, chi_dev, owners, capacity):
    owner = partial_target_tile // chi_dev
    member = (owner[:, None] == jnp.arange(owners, dtype=jnp.int32)[None, :]).astype(jnp.int32)
    before = jnp.cumsum(member, axis=0) - member
    rank = jnp.sum(before * member, axis=1)
    position = owner * capacity + rank
    places = jnp.arange(owners * capacity, dtype=jnp.int32)
    match = position[:, None] == places[None, :]
    filled = jnp.any(match, axis=0)
    source = jnp.sum(
        jnp.where(match, jnp.arange(partial_target_tile.shape[0], dtype=jnp.int32)[:, None], 0),
        axis=0,
    )
    local = jnp.sum(jnp.where(match, (partial_target_tile % chi_dev)[:, None], 0), axis=0)
    slot_ids = jnp.where(filled, local, -1).astype(jnp.float32)
    return (source, filled, slot_ids)


def body(occupied, virtual, cos_weights, pair_occ, pair_virt, partial_target_tile):
    owners = lax.axis_size("tile")
    groups = lax.axis_size("tau")
    part_count = pair_occ.shape[0]
    capacity = 2 * part_count // owners
    chi_dev = CHI_DEV
    tau_count = occupied.shape[0]
    tile_size = occupied.shape[2]
    source, filled, slot_ids = slot_layout(partial_target_tile, chi_dev, owners, capacity)
    mask = filled.astype(jnp.float32)
    rows = tile_size // groups
    partial_value = block_products(occupied, virtual, pair_occ, pair_virt, groups)
    slots = source.shape[0]
    outgoing = jnp.take(partial_value, source, axis=1) * mask[None, :, None, None, None]
    split_rows = outgoing.reshape(groups * slots, tau_count, rows, tile_size)
    repeated_ids = jnp.tile(slot_ids, groups)
    incoming, arrived = in_one_piece((split_rows, repeated_ids), ("tau", "tile"), 0, 0, 1)
    incoming = incoming.reshape(groups, slots, tau_count * rows * tile_size)
    arrived = arrived.reshape(groups, slots)
    selector = (
        arrived[:, None, :] == jnp.arange(chi_dev, dtype=jnp.float32)[None, :, None]
    ).astype(jnp.float32)
    chi_time = jnp.einsum("xcs,xsf->cxf", selector, incoming, precision=lax.Precision.HIGHEST)
    chi_time = chi_time.reshape(chi_dev, groups * tau_count, rows, tile_size)
    return jnp.einsum("kt,ctrd->kcrd", cos_weights, chi_time, precision=lax.Precision.HIGHEST)


def solution(mesh):
    in_specs = (
        P("tau", "tile", None, None),
        P("tau", "tile", None, None),
        P(),
        P("tile", None),
        P("tile", None),
        P("tile"),
    )
    out_specs = P(None, "tile", "tau", None)
    return jax.shard_map(body, mesh=mesh, in_specs=in_specs, out_specs=out_specs, check_vma=False)
```

profile of v0, /device:TPU:0, one launch (start us, length us, event | category | flops | bytes accessed | tf_op | source)
XLA Modules:
  0.0 955.3 jit_solution(7878079829436881421)
XLA Ops:
  4.7 6.2 broadcast_in_dim.61
  10.8 504.4 %while.13 = (s32[]{:T(128)}, f32[8,192,1,16,128]{4,3,0,1,2:T(8,128)}, bf16[1,128,128,128]{3,2,1,0:T(8,128)(2,1)}, s32[192,16]{1,0:T(8,128)S(1)}, bf16[1,128,128,...) while((s32[]{:T(128)}, ...), condition=%wide.region_5.7_spmd, body=%wide.region_4.6_spmd.sunk | while | flops 541068800 | bytes 34093720 | solution.py:47
  11.0 5.2 gather_fusion
  26.1 5.8 fusion.31
  32.1 5.2 gather_fusion
  47.1 5.8 fusion.31
  53.2 5.2 gather_fusion
  68.2 5.8 fusion.31
  74.2 5.2 gather_fusion
  89.2 5.8 fusion.31
  95.2 5.2 gather_fusion
  110.2 5.8 fusion.31
  131.2 5.8 fusion.31
  137.2 5.2 gather_fusion
  152.3 5.8 fusion.31
  173.2 5.8 fusion.31
  179.2 5.2 gather_fusion
  194.3 5.8 fusion.31
  200.2 5.2 gather_fusion
  215.3 5.8 fusion.31
  236.3 5.8 fusion.31
  242.3 5.2 gather_fusion
  257.3 5.8 fusion.31
  263.3 5.2 gather_fusion
  278.3 5.8 fusion.31
  284.3 5.2 gather_fusion
  299.4 5.8 fusion.31
  305.3 5.2 gather_fusion
  320.4 5.8 fusion.31
  341.4 5.8 fusion.31
  347.3 5.2 gather_fusion
  362.4 5.8 fusion.31
  383.4 5.8 fusion.31
  389.4 5.2 gather_fusion
  404.4 5.8 fusion.31
  425.4 5.8 fusion.31
  446.4 5.8 fusion.31
  467.4 5.8 fusion.31
  488.4 5.8 fusion.31
  509.4 5.8 fusion.31
  515.2 19.3 %gather_fusion.2 = f32[384,8,16,128]{3,2,1,0:T(8,128)} fusion(f32[8,192,16,128]{3,2,0,1:T(8,128)} %bitcast.82, s32[1024]{0:T(1024)S(1)} %pad_clamp_fusion.2), kind=kCustom, calls=%fused_computation.2 | custom fusion | bytes 50333184 | tf_op jit(solution)/shard_map/jit(_take)/gather | solution.py:81
  534.5 17.2 %copy.37 = f32[8,384,16,128]{3,2,1,0:T(8,128)} copy(f32[8,384,16,128]{3,2,0,1:T(8,128)} %bitcast.90) | data formatting | bytes 50331648 | tf_op jit(solution)/shard_map/jit(_take)/gather | solution.py:81
  551.8 26.8 %gather.10 = f32[128,24,2048]{2,1,0:T(8,128)} reshape(f32[8,384,16,128]{3,2,1,0:T(8,128)} %copy.37) | data formatting | bytes 50331648 | tf_op jit(solution)/shard_map/jit(_take)/gather | solution.py:81
  578.5 17.3 %select_multiply_fusion = f32[128,24,2048]{2,1,0:T(8,128)} fusion(f32[128,24,2048]{2,1,0:T(8,128)} %gather.10, f32[128,24]{1,0:T(8,128)S(1)} %bitcast.93, pred[128,24]{1,0:T(8,128)(4,1)S(1)} %bitcast.94), kind=kLoop, calls=%fused_computation.19 | loop fusion | flops 12582912 | bytes 50347008 | tf_op jit(solution)/shard_map/mul | solution.py:81
  595.8 9.4 pad_maximum_fusion
  605.2 312.4 %all_to_all.9 = f32[128,24,2049]{2,1,0:T(8,128)} all-to-all(f32[128,24,2049]{2,1,0:T(8,128)S(1)} %pad_maximum_fusion), channel_id=1, replica_groups=mesh['tau'=8,'tile'=16] {'tau','tile'}, dimensions={0} | all-to-all | bytes 50356224 | tf_op jit(solution)/shard_map/all_to_all | solution.py:15
  919.5 17.4 %slice.28 = f32[3072,2048]{1,0:T(8,128)} slice(f32[3072,2049]{1,0:T(8,128)} %bitcast.84), slice={[0:3072], [0:2048]} | slice | bytes 50331648 | tf_op jit(solution)/shard_map/slice | solution.py:20
  936.9 13.9 %fusion.17 = f32[8,2048,32]{1,2,0:T(8,128)S(1)} fusion(f32[8,384,2048]{2,1,0:T(8,128)} %bitcast.89, f32[8,384]{1,0:T(8,128)S(1)} %eq.59), kind=kOutput, calls=%fused_computation.25 | convolution fusion | flops 2416017408 | bytes 27275264 | tf_op jit(solution)/shard_map/xcs,xsf->cxf/dot_general | solution.py:90
  (213 shorter events, 302.9 us)
Async XLA Ops:
  0.0 951.1 %copy-start = (f32[4,8]{1,0:T(4,128)S(1)}, f32[4,8]{1,0:T(4,128)}, u32[]{:S(2)}) copy-start(f32[4,8]{1,0:T(4,128)} %param.12) | copy-start | bytes 388
where the time goes:
time: 962 us; the launch traced here: 955 us
  local copies, waits for them, and re-layouts  348 us (36%)
  blocking collectives  312 us (32%)
  matrix products  156 us (16%)
  other arithmetic  138 us (14%)
    all_to_all x1, blocking collectives, in_one_piece(): lax.all_to_all(both, axis, split_axis=split_dim, concat_axis=concat_dim,...  312 us
    dot_general x24, matrix products, one_block(): jnp.einsum('bjgrk,bjkc->gbrc', left, right, preferred_element_type=jnp.fl...  139 us
    gather x24, local copies, waits for them, and re-layouts, one_block(): left = jnp.take(occupied[0], occ_rows, axis=0)  126 us
    gather x24, local copies, waits for them, and re-layouts, one_block(): right = jnp.take(virtual[0], virt_rows, axis=0)  126 us
    select_n x24, other arithmetic, one_block(): left = jnp.take(occupied[0], occ_rows, axis=0)  109 us
    gather x3, local copies, waits for them, and re-layouts, body(): jnp.take(partial_value, source, axis=1) * mask[None, :, None, None, None]  63.3 us
    slice x2, local copies, waits for them, and re-layouts, in_one_piece(): piece = out[..., at:at + column.shape[along]]  19.3 us

commit v1 on v0

v1 whole, which is shorter than its diff:
```python
import jax
import jax.numpy as jnp
from jax import lax
from jax.experimental import pallas as pl
from jax.experimental.pallas import tpu as pltpu
from jax.sharding import PartitionSpec as P

TILE = 128
SUB = 8
CHI_DEV = 32


def product_kernel(occ_index, virt_index, occupied, virtual, out, *, terms):
    first = pl.program_id(0) * SUB
    flat = out.reshape(TILE * SUB, TILE)
    for q in range(SUB):
        base = (first + q) * terms
        left = jnp.concatenate([occupied[occ_index[base + j]] for j in range(terms)], axis=1)
        right = jnp.concatenate([virtual[virt_index[base + j]] for j in range(terms)], axis=0)
        product = jnp.dot(left, right, preferred_element_type=jnp.float32)
        for i in range(TILE // SUB):
            flat[pl.ds(i * SUB * SUB + q, SUB, stride=SUB), :] = product[i * SUB : (i + 1) * SUB]


def products(occ_index, virt_index, occupied, virtual):
    part, terms = occ_index.shape
    whole = pl.BlockSpec(occupied.shape, lambda g, *_: (0, 0, 0))

    def kernel(*refs):
        product_kernel(*refs, terms=terms)

    return pl.pallas_call(
        kernel,
        out_shape=jax.ShapeDtypeStruct((TILE, part, TILE), jnp.float32),
        grid_spec=pltpu.PrefetchScalarGridSpec(
            num_scalar_prefetch=2,
            grid=(part // SUB,),
            in_specs=[whole, whole],
            out_specs=pl.BlockSpec((TILE, SUB, TILE), lambda g, *_: (0, g, 0)),
        ),
        compiler_params=pltpu.CompilerParams(vmem_limit_bytes=48 * 2**20),
        name="products",
    )(occ_index.reshape(-1), virt_index.reshape(-1), occupied, virtual)


def response_kernel(target, weights, rows, out, even, odd, *, part, chi, nfreq, ntau):
    block = pl.program_id(0)

    @pl.when(block == 0)
    def _():
        even[...] = jnp.zeros_like(even)
        odd[...] = jnp.zeros_like(odd)

    def add(g, carry):
        at = pl.multiple_of(g * SUB, SUB)
        piece = jnp.swapaxes(rows[:, pl.ds(at, SUB), :], 0, 1)
        for q in range(SUB):
            acc = odd if q % 2 else even
            tile = target[block * part + at + q]
            acc[tile] += piece[q]
        return carry

    lax.fori_loop(0, part // SUB, add, 0)

    @pl.when(block == pl.num_programs(0) - 1)
    def _():
        def transform(g, carry):
            at = pl.multiple_of(g * SUB, SUB)
            total = even[pl.ds(at, SUB)] + odd[pl.ds(at, SUB)]
            times = jnp.swapaxes(total, 0, 1)
            owner = g // (CHI_DEV // SUB)
            place = pl.multiple_of((g % (CHI_DEV // SUB)) * SUB, SUB)
            for k in range(nfreq):
                value = weights[k * ntau] * times[0]
                for t in range(1, ntau):
                    value = value + weights[k * ntau + t] * times[t]
                out[owner, k, pl.ds(place, SUB), :] = value
            return carry

        lax.fori_loop(0, chi // SUB, transform, 0)


def responses(target, weights, rows):
    ntau, blocks, part, width = rows.shape
    nfreq = weights.shape[0]
    chi = blocks * CHI_DEV

    def kernel(*refs):
        response_kernel(*refs, part=part, chi=chi, nfreq=nfreq, ntau=ntau)

    return pl.pallas_call(
        kernel,
        out_shape=jax.ShapeDtypeStruct((blocks, nfreq, CHI_DEV, width), jnp.float32),
        grid_spec=pltpu.PrefetchScalarGridSpec(
            num_scalar_prefetch=2,
            grid=(blocks,),
            in_specs=[pl.BlockSpec((ntau, None, part, width), lambda b, *_: (0, b, 0, 0))],
            out_specs=pl.BlockSpec((blocks, nfreq, CHI_DEV, width), lambda b, *_: (0, 0, 0, 0)),
            scratch_shapes=[pltpu.VMEM((chi, ntau, width), jnp.float32)] * 2,
        ),
        compiler_params=pltpu.CompilerParams(vmem_limit_bytes=48 * 2**20),
        name="responses",
    )(target, weights.reshape(-1), rows)


def body(occupied, virtual, cos_weights, pair_occ, pair_virt, partial_target_tile):
    ntau = lax.axis_size("tau")
    blocks = lax.axis_size("tile")
    target = lax.all_gather(partial_target_tile, "tile", tiled=True)
    value = products(pair_occ, pair_virt, occupied[0], virtual[0])
    rows = lax.all_to_all(value, ("tau", "tile"), 0, 0, tiled=True)
    rows = rows.reshape(ntau, blocks, *rows.shape[1:])
    spectrum = responses(target, cos_weights, rows)
    owned = lax.all_to_all(spectrum, "tile", 0, 0, tiled=True)
    return jnp.transpose(owned, (1, 2, 0, 3))


def solution(mesh):
    in_specs = (
        P("tau", "tile", None, None),
        P("tau", "tile", None, None),
        P(),
        P("tile", None),
        P("tile", None),
        P("tile"),
    )
    out_specs = P(None, "tile", "tau", None)
    return jax.shard_map(body, mesh=mesh, in_specs=in_specs, out_specs=out_specs, check_vma=False)
```

time: 962 us -> 305 us (0.32)
  local copies, waits for them, and re-layouts: 348 us -> 6.54 us
  matrix products: 156 us -> 0 us
  other arithmetic: 138 us -> 0 us
  blocking collectives: 312 us -> 234 us
  Pallas kernels: 0 us -> 51.5 us
  starting transfers between devices: 0 us -> 11.6 us
    gather x51 -> x0, local copies, waits for them, and re-layouts: 315 us -> none  [the longest x24 126 us: one_block(): left = jnp.take(occupied[0], occ_rows, axis=0)]
    all_to_all x1, blocking collectives: 312 us -> 15.6 us  [body(): owned = lax.all_to_all(spectrum, 'tile', 0, 0, tiled=True)]
    unnamed x0 -> x1, blocking collectives: none -> 219 us
    dot_general x26 -> x0, matrix products: 156 us -> none  [the longest x24 139 us: one_block(): jnp.einsum('bjgrk,bjkc->gbrc', left, right, preferred_element_type=jnp.fl...]
    select_n x26 -> x0, other arithmetic: 110 us -> none  [the longest x24 109 us: one_block(): left = jnp.take(occupied[0], occ_rows, axis=0)]
    pallas_call x0 -> x2, Pallas kernels: none -> 51.5 us  [the longest x1 34.4 us: products(): pl.pallas_call(kernel, out_shape=jax.ShapeDtypeStruct((TILE, part, TILE),...]
    slice x3 -> x0, local copies, waits for them, and re-layouts: 19.5 us -> none  [the longest x2 19.3 us: in_one_piece(): piece = out[..., at:at + column.shape[along]]]
    mul x1 -> x0, other arithmetic: 17.3 us -> none  [body(): jnp.take(partial_value, source, axis=1) * mask[None, :, None, None, None]]
  transfers between devices with their start and end apart: 0 -> 1, of which waited for: 0 -> 0; matrix products, arithmetic and copies ran while one was open for 0% -> 0% of each run, Pallas kernels for 0% -> 0%
where the time goes in v1:
time: 305 us; the launch traced here: 304 us
  blocking collectives  234 us (77%)
  Pallas kernels  51.5 us (17%)
  starting transfers between devices  11.6 us (4%)
  local copies, waits for them, and re-layouts  6.54 us (2%)
    unnamed x1, blocking collectives  219 us
    pallas_call x1, Pallas kernels, products(): pl.pallas_call(kernel, out_shape=jax.ShapeDtypeStruct((TILE, part, TILE),...  34.4 us
    pallas_call x1, Pallas kernels, responses(): pl.pallas_call(kernel, out_shape=jax.ShapeDtypeStruct((blocks, nfreq, CHI...  17 us
    all_to_all x1, blocking collectives, body(): owned = lax.all_to_all(spectrum, 'tile', 0, 0, tiled=True)  15.6 us
    all_to_all x1, starting transfers between devices, body(): rows = lax.all_to_all(value, ('tau', 'tile'), 0, 0, tiled=True)  11.6 us
  transfers between devices with their start and end apart: 1, of which 0 were waited for; matrix products, arithmetic and copies ran while one was open for 0% of the time, Pallas kernels for 0%

profile of v1, /device:TPU:0, one launch (start us, length us, event | category | flops | bytes accessed | tf_op | source)
XLA Modules:
  0.0 304.5 jit_solution(734142308782924366)
XLA Ops:
  0.0 0.8 copy.8
  0.8 0.1 reshape.13.refs_0_
  0.9 0.8 copy.9
  1.7 0.1 reshape.14.refs_1_
  1.8 0.0 copy-start
  1.8 2.2 copy-done
  4.0 34.4 %products.1 = f32[128,192,128]{2,1,0:T(8,128)} custom-call(s32[3072]{0:T(1024)S(1)} %reshape.13.refs_0_, s32[3072]{0:T(1024)S(1)} %reshape.14.refs_1_, bf16[128,128,128]{2,1,0:T(8,128)(2,1)S(1)} %bitcast.5, bf16[128,128,128]{2,1,0:T(8,128)(2,1)} %bitcast.7), custom_call_target="tpu_custom_call" | custom-call | tf_op jit(solution)/shard_map/products/pallas_call | solution.py:32
  38.5 0.0 copy-start.1
  38.5 0.0 copy-start.3
  38.5 0.0 copy-start.2
  38.5 11.6 %all-to-all-start = ((f32[128,192,128]{2,1,0:T(8,128)}), f32[128,192,128]{2,1,0:T(8,128)}, u32[]{:S(2)}, u32[]{:S(2)}) async-start(f32[128,192,128]{2,1,0:T(8,128)} %products.1), calls=%async_computation | async-start | bytes 25165824 | tf_op jit(solution)/shard_map/all_to_all | solution.py:111
  50.1 0.0 copy-done.1
  50.1 0.1 reshape.12.refs_1_
  50.2 0.0 copy-done.3
  50.2 0.6 dynamic-slice
  51.5 0.0 copy-done.2
  51.5 0.3 dynamic-update-slice
  51.8 218.5 %all-reduce.refs_0_ = s32[3072]{0:T(1024)S(1)} all-reduce(s32[3072]{0:T(1024)S(1)} %dynamic-update-slice), channel_id=1, replica_groups=mesh['tau'=8,'tile'=16] {'tile'}, use_global_device_ids=true, to_apply=%add | all-reduce | flops 3072 | bytes 24576
  270.3 0.0 all-to-all-done
  270.3 17.0 %responses.1 = f32[16,4,32,128]{3,2,1,0:T(8,128)S(1)} custom-call(s32[3072]{0:T(1024)S(1)} %all-reduce.refs_0_, f32[32]{0:T(128)S(1)} %reshape.12.refs_1_, f32[8,16,192,128]{3,2,1,0:T(8,128)} %bitcast.3.refs_2_), custom_call_target="tpu_custom_call" | custom-call | tf_op jit(solution)/shard_map/responses/pallas_call | solution.py:91
  287.3 15.6 %all_to_all.10 = f32[16,4,32,128]{3,2,1,0:T(8,128)S(1)} all-to-all(f32[16,4,32,128]{3,2,1,0:T(8,128)S(1)} %responses.1), channel_id=1, replica_groups=mesh['tau'=8,'tile'=16] {'tile'}, dimensions={0} | all-to-all | bytes 2097152 | tf_op jit(solution)/shard_map/all_to_all | solution.py:114
  302.9 1.6 copy.10
  (1 shorter events, 0.0 us)
Async XLA Ops:
  1.8 2.2 copy-start
  38.5 11.7 %copy-start.1 = (f32[4,8]{1,0:T(4,128)S(1)}, f32[4,8]{1,0:T(4,128)}, u32[]{:S(2)}) copy-start(f32[4,8]{1,0:T(4,128)} %param.8) | copy-start | bytes 388
  38.5 11.8 %copy-start.3 = (u32[128]{0:T(128)S(1)}, u32[128]{0:T(128)}, u32[]{:S(2)}) copy-start(u32[128]{0:T(128)} %constant.4) | copy-start | bytes 1540
  38.5 13.0 %copy-start.2 = (s32[192]{0:T(256)S(1)}, s32[192]{0:T(256)}, u32[]{:S(2)}) copy-start(s32[192]{0:T(256)} %param.11) | copy-start | bytes 2308
  38.5 231.8 %all-to-all-start = ((f32[128,192,128]{2,1,0:T(8,128)}), f32[128,192,128]{2,1,0:T(8,128)}, u32[]{:S(2)}, u32[]{:S(2)}) async-start(f32[128,192,128]{2,1,0:T(8,128)} %products.1), calls=%async_computation | async-start | bytes 25165824 | tf_op jit(solution)/shard_map/all_to_all | solution.py:111

commit v2 on v1

v2 whole, which is shorter than its diff:
```python
import jax
import jax.numpy as jnp
from jax import lax
from jax.experimental import pallas as pl
from jax.experimental.pallas import tpu as pltpu
from jax.sharding import PartitionSpec as P

TILE = 128
SUB = 8
CHI_DEV = 32


def product_kernel(occ_index, virt_index, occupied, virtual, out, *, terms, start):
    first = start + pl.program_id(0) * SUB
    flat = out.reshape(TILE * SUB, TILE)
    for q in range(SUB):
        base = (first + q) * terms
        left = jnp.concatenate([occupied[occ_index[base + j]] for j in range(terms)], axis=1)
        right = jnp.concatenate([virtual[virt_index[base + j]] for j in range(terms)], axis=0)
        product = jnp.dot(left, right, preferred_element_type=jnp.float32)
        for i in range(TILE // SUB):
            flat[pl.ds(i * SUB * SUB + q, SUB, stride=SUB), :] = product[i * SUB : (i + 1) * SUB]


def products(occ_index, virt_index, occupied, virtual, start, part, terms):
    whole = pl.BlockSpec(occupied.shape, lambda g, *_: (0, 0, 0))

    def kernel(*refs):
        product_kernel(*refs, terms=terms, start=start)

    return pl.pallas_call(
        kernel,
        out_shape=jax.ShapeDtypeStruct((TILE, part, TILE), jnp.float32),
        grid_spec=pltpu.PrefetchScalarGridSpec(
            num_scalar_prefetch=2,
            grid=(part // SUB,),
            in_specs=[whole, whole],
            out_specs=pl.BlockSpec((TILE, SUB, TILE), lambda g, *_: (0, g, 0)),
        ),
        compiler_params=pltpu.CompilerParams(vmem_limit_bytes=48 * 2**20),
        name="products",
    )(occ_index, virt_index, occupied, virtual)


def add_kernel(target, rows, *refs, first, part, stride):
    *given, out, even, odd = refs
    block = pl.program_id(0)

    @pl.when(block == 0)
    def _():
        even[...] = given[0][...] if given else jnp.zeros_like(even)
        odd[...] = jnp.zeros_like(odd)

    def add(g, carry):
        at = pl.multiple_of(g * SUB, SUB)
        piece = jnp.swapaxes(rows[:, pl.ds(at, SUB), :], 0, 1)
        for q in range(SUB):
            acc = odd if q % 2 else even
            tile = target[block * stride + first + at + q]
            acc[tile] += piece[q]
        return carry

    lax.fori_loop(0, part // SUB, add, 0)

    @pl.when(block == pl.num_programs(0) - 1)
    def _():
        out[...] = even[...] + odd[...]


def add_rows(target, rows, given, first, stride):
    ntau, blocks, part, width = rows.shape
    chi = (blocks * CHI_DEV, ntau, width)
    whole = pl.BlockSpec(chi, lambda b, *_: (0, 0, 0))

    def kernel(*refs):
        add_kernel(*refs, first=first, part=part, stride=stride)

    return pl.pallas_call(
        kernel,
        out_shape=jax.ShapeDtypeStruct(chi, jnp.float32),
        grid_spec=pltpu.PrefetchScalarGridSpec(
            num_scalar_prefetch=1,
            grid=(blocks,),
            in_specs=[pl.BlockSpec((ntau, None, part, width), lambda b, *_: (0, b, 0, 0))] + [whole] * len(given),
            out_specs=whole,
            scratch_shapes=[pltpu.VMEM(chi, jnp.float32)] * 2,
        ),
        compiler_params=pltpu.CompilerParams(vmem_limit_bytes=48 * 2**20),
        name="add_rows",
    )(target, rows, *given)


def transform_kernel(weights, chi, out, *, nfreq, ntau):
    def step(g, carry):
        at = pl.multiple_of(g * SUB, SUB)
        times = jnp.swapaxes(chi[pl.ds(at, SUB)], 0, 1)
        owner = g // (CHI_DEV // SUB)
        place = pl.multiple_of((g % (CHI_DEV // SUB)) * SUB, SUB)
        for k in range(nfreq):
            value = weights[k * ntau] * times[0]
            for t in range(1, ntau):
                value = value + weights[k * ntau + t] * times[t]
            out[owner, k, pl.ds(place, SUB), :] = value
        return carry

    lax.fori_loop(0, chi.shape[0] // SUB, step, 0)


def transform(weights, chi):
    tiles, ntau, width = chi.shape
    nfreq = weights.shape[0]
    shape = (tiles // CHI_DEV, nfreq, CHI_DEV, width)

    def kernel(*refs):
        transform_kernel(*refs, nfreq=nfreq, ntau=ntau)

    return pl.pallas_call(
        kernel,
        out_shape=jax.ShapeDtypeStruct(shape, jnp.float32),
        grid_spec=pltpu.PrefetchScalarGridSpec(
            num_scalar_prefetch=1,
            grid=(1,),
            in_specs=[pl.BlockSpec(chi.shape, lambda b, *_: (0, 0, 0))],
            out_specs=pl.BlockSpec(shape, lambda b, *_: (0, 0, 0, 0)),
        ),
        compiler_params=pltpu.CompilerParams(vmem_limit_bytes=48 * 2**20),
        name="transform",
    )(weights.reshape(-1), chi)


CHUNKS = (48, 96, 48)


def body(occupied, virtual, cos_weights, pair_occ, pair_virt, partial_target_tile):
    ntau = lax.axis_size("tau")
    blocks = lax.axis_size("tile")
    part, terms = pair_occ.shape
    copies = jnp.broadcast_to(partial_target_tile, (blocks, part))
    target = lax.all_to_all(copies, "tile", 0, 0, tiled=True).reshape(-1)
    target, occ_index, virt_index = lax.optimization_barrier((target, pair_occ.reshape(-1), pair_virt.reshape(-1)))
    first = 0
    arrived = []
    for count in CHUNKS:
        value = products(occ_index, virt_index, occupied[0], virtual[0], first, count, terms)
        rows = lax.all_to_all(value, ("tau", "tile"), 0, 0, tiled=True)
        arrived.append((first, rows.reshape(ntau, blocks, *rows.shape[1:])))
        first += count
    chi = ()
    for first, rows in arrived:
        chi = (add_rows(target, rows, chi, first, part),)
    spectrum = transform(cos_weights, chi[0])
    owned = lax.all_to_all(spectrum, "tile", 0, 0, tiled=True)
    return jnp.transpose(owned, (1, 2, 0, 3))


def solution(mesh):
    in_specs = (
        P("tau", "tile", None, None),
        P("tau", "tile", None, None),
        P(),
        P("tile", None),
        P("tile", None),
        P("tile"),
    )
    out_specs = P(None, "tile", "tau", None)
    return jax.shard_map(body, mesh=mesh, in_specs=in_specs, out_specs=out_specs, check_vma=False)
```

time: 305 us -> 245 us (0.80)
  blocking collectives: 234 us -> 20.7 us
  waiting for transfers between devices: 0.01 us -> 115 us
  Pallas kernels: 51.5 us -> 71.8 us
  starting transfers between devices: 11.6 us -> 25.9 us
  local copies, waits for them, and re-layouts: 6.54 us -> 10.3 us
    unnamed x1 -> x0, blocking collectives: 219 us -> none
    all_to_all x1 -> x3, waiting for transfers between devices: 0.01 us -> 109 us  [body(): rows = lax.all_to_all(value, ('tau', 'tile'), 0, 0, tiled=True)]
    pallas_call x1 -> x4, Pallas kernels: 17 us -> 28.2 us  [the longest x3 25.9 us: add_rows(): pl.pallas_call(kernel, out_shape=jax.ShapeDtypeStruct(chi, jnp.float32),...]
    pallas_call x1 -> x3, Pallas kernels: 34.4 us -> 43.6 us  [products(): pl.pallas_call(kernel, out_shape=jax.ShapeDtypeStruct((TILE, part, TILE),...]
    all_to_all x0 -> x1, starting transfers between devices: none -> 8.16 us  [body(): target = lax.all_to_all(copies, 'tile', 0, 0, tiled=True).reshape(-1)]
    all_to_all x1 -> x3, starting transfers between devices: 11.6 us -> 17.8 us  [body(): rows = lax.all_to_all(value, ('tau', 'tile'), 0, 0, tiled=True)]
    all_to_all x0 -> x1, waiting for transfers between devices: none -> 5.76 us  [body(): target = lax.all_to_all(copies, 'tile', 0, 0, tiled=True).reshape(-1)]
    all_to_all x1, blocking collectives: 15.6 us -> 20.7 us  [body(): owned = lax.all_to_all(spectrum, 'tile', 0, 0, tiled=True)]
  transfers between devices with their start and end apart: 1 -> 4, of which waited for: 0 -> 4; matrix products, arithmetic and copies ran while one was open for 0% -> 1% of each run, Pallas kernels for 0% -> 19%
where the time goes in v2:
time: 245 us; the launch traced here: 244 us
  waiting for transfers between devices  115 us (47%)
  Pallas kernels  71.8 us (29%)
  starting transfers between devices  25.9 us (11%)
  blocking collectives  20.7 us (8%)
  local copies, waits for them, and re-layouts  10.3 us (4%)
    all_to_all x3, waiting for transfers between devices, body(): rows = lax.all_to_all(value, ('tau', 'tile'), 0, 0, tiled=True)  109 us
    pallas_call x3, Pallas kernels, products(): pl.pallas_call(kernel, out_shape=jax.ShapeDtypeStruct((TILE, part, TILE),...  43.6 us
    pallas_call x3, Pallas kernels, add_rows(): pl.pallas_call(kernel, out_shape=jax.ShapeDtypeStruct(chi, jnp.float32),...  25.9 us
    all_to_all x1, blocking collectives, body(): owned = lax.all_to_all(spectrum, 'tile', 0, 0, tiled=True)  20.7 us
    all_to_all x3, starting transfers between devices, body(): rows = lax.all_to_all(value, ('tau', 'tile'), 0, 0, tiled=True)  17.8 us
    all_to_all x1, starting transfers between devices, body(): target = lax.all_to_all(copies, 'tile', 0, 0, tiled=True).reshape(-1)  8.16 us
    unnamed x10, local copies, waits for them, and re-layouts  7.08 us
    all_to_all x1, waiting for transfers between devices, body(): target = lax.all_to_all(copies, 'tile', 0, 0, tiled=True).reshape(-1)  5.76 us
  transfers between devices with their start and end apart: 4, of which 4 were waited for; matrix products, arithmetic and copies ran while one was open for 1% of the time, Pallas kernels for 19%

profile of v2, /device:TPU:0, one launch (start us, length us, event | category | flops | bytes accessed | tf_op | source)
XLA Modules:
  0.0 243.6 jit_solution(11635433308284338984)
XLA Ops:
  0.0 1.3 broadcast_in_dim.3
  1.3 8.2 %all-to-all-start = ((s32[16,1,192]{2,1,0:T(1,128)}), s32[16,1,192]{2,1,0:T(1,128)S(1)}, u32[]{:S(2)}, u32[]{:S(2)}) async-start(s32[16,1,192]{2,1,0:T(1,128)} %broadcast_in_dim.3), calls=%async_computation | async-start | bytes 32768 | tf_op jit(solution)/shard_map/all_to_all | solution.py:139
  9.5 0.8 copy.8
  10.3 0.1 reshape.28.refs_0_
  10.4 0.8 copy.9
  11.2 0.1 reshape.29.refs_1_
  11.3 5.8 %all-to-all-done = s32[16,1,192]{2,1,0:T(1,128)S(1)} async-done(((s32[16,1,192]{2,1,0:T(1,128)}), s32[16,1,192]{2,1,0:T(1,128)S(1)}, u32[]{:S(2)}, u32[]{:S(2)}) %all-to-all-start) | async-done | bytes 12320 | tf_op jit(solution)/shard_map/all_to_all | solution.py:139
  17.1 0.1 reshape.27.refs_0_
  17.2 12.2 %products.5 = f32[128,48,128]{2,1,0:T(8,128)S(1)} custom-call(s32[3072]{0:T(1024)S(1)} %reshape.28.refs_0_, s32[3072]{0:T(1024)S(1)} %reshape.29.refs_1_, bf16[128,128,128]{2,1,0:T(8,128)(2,1)} %bitcast.6, bf16[128,128,128]{2,1,0:T(8,128)(2,1)} %bitcast.10), custom_call_target="tpu_custom_call" | custom-call | tf_op jit(solution)/shard_map/products/pallas_call | solution.py:31
  29.4 0.0 copy-start.2
  29.4 1.6 copy-done.2
  31.0 6.2 %all-to-all-start.3 = ((f32[128,48,128]{2,1,0:T(8,128)}), f32[128,48,128]{2,1,0:T(8,128)S(1)}, u32[]{:S(2)}, u32[]{:S(2)}) async-start(f32[128,48,128]{2,1,0:T(8,128)} %copy-done.2), calls=%async_computation.3 | async-start | bytes 6291456 | tf_op jit(solution)/shard_map/all_to_all | solution.py:145
  37.3 0.0 copy-start
  37.3 2.2 copy-done
  39.4 19.2 %products.4 = f32[128,96,128]{2,1,0:T(8,128)} custom-call(s32[3072]{0:T(1024)S(1)} %reshape.28.refs_0_, s32[3072]{0:T(1024)S(1)} %reshape.29.refs_1_, bf16[128,128,128]{2,1,0:T(8,128)(2,1)S(1)} %bitcast.8, bf16[128,128,128]{2,1,0:T(8,128)(2,1)} %bitcast.11), custom_call_target="tpu_custom_call" | custom-call | tf_op jit(solution)/shard_map/products/pallas_call | solution.py:31
  58.7 19.0 %all-to-all-done.3 = f32[128,48,128]{2,1,0:T(8,128)S(1)} async-done(((f32[128,48,128]{2,1,0:T(8,128)}), f32[128,48,128]{2,1,0:T(8,128)S(1)}, u32[]{:S(2)}, u32[]{:S(2)}) %all-to-all-start.3) | async-done | bytes 3145760 | tf_op jit(solution)/shard_map/all_to_all | solution.py:145
  77.7 5.8 %all-to-all-start.2 = ((f32[128,96,128]{2,1,0:T(8,128)}), f32[128,96,128]{2,1,0:T(8,128)}, u32[]{:S(2)}, u32[]{:S(2)}) async-start(f32[128,96,128]{2,1,0:T(8,128)} %products.4), calls=%async_computation.2 | async-start | bytes 12582912 | tf_op jit(solution)/shard_map/all_to_all | solution.py:145
  83.5 12.2 %products.3 = f32[128,48,128]{2,1,0:T(8,128)S(1)} custom-call(s32[3072]{0:T(1024)S(1)} %reshape.28.refs_0_, s32[3072]{0:T(1024)S(1)} %reshape.29.refs_1_, bf16[128,128,128]{2,1,0:T(8,128)(2,1)} %bitcast.7, bf16[128,128,128]{2,1,0:T(8,128)(2,1)} %bitcast.12), custom_call_target="tpu_custom_call" | custom-call | tf_op jit(solution)/shard_map/products/pallas_call | solution.py:31
  95.7 0.0 copy-start.1
  95.7 1.6 copy-done.1
  97.3 0.0 copy-start.3
  97.3 65.8 %all-to-all-done.2 = f32[128,96,128]{2,1,0:T(8,128)} async-done(((f32[128,96,128]{2,1,0:T(8,128)}), f32[128,96,128]{2,1,0:T(8,128)}, u32[]{:S(2)}, u32[]{:S(2)}) %all-to-all-start.2) | async-done | bytes 6291488 | tf_op jit(solution)/shard_map/all_to_all | solution.py:145
  163.1 5.7 %all-to-all-start.1 = ((f32[128,48,128]{2,1,0:T(8,128)}), f32[128,48,128]{2,1,0:T(8,128)}, u32[]{:S(2)}, u32[]{:S(2)}) async-start(f32[128,48,128]{2,1,0:T(8,128)} %copy-done.1), calls=%async_computation.1 | async-start | bytes 6291456 | tf_op jit(solution)/shard_map/all_to_all | solution.py:145
  168.9 0.0 copy-done.3
  168.9 0.1 reshape.26.refs_0_
  168.9 3.8 %add_rows.3.refs_2_ = f32[512,8,128]{2,1,0:T(8,128)S(1)} custom-call(s32[3072]{0:T(1024)S(1)} %reshape.27.refs_0_, f32[8,16,48,128]{3,2,1,0:T(8,128)S(1)} %bitcast.9), custom_call_target="tpu_custom_call" | custom-call | tf_op jit(solution)/shard_map/add_rows/pallas_call | solution.py:78
  172.8 11.9 %add_rows.4.refs_2_ = f32[512,8,128]{2,1,0:T(8,128)S(1)} custom-call(s32[3072]{0:T(1024)S(1)} %reshape.27.refs_0_, f32[8,16,96,128]{3,2,1,0:T(8,128)} %bitcast.3.refs_1_, f32[512,8,128]{2,1,0:T(8,128)S(1)} %add_rows.3.refs_2_), custom_call_target="tpu_custom_call" | custom-call | tf_op jit(solution)/shard_map/add_rows/pallas_call | solution.py:78
  184.8 24.1 %all-to-all-done.1 = f32[128,48,128]{2,1,0:T(8,128)} async-done(((f32[128,48,128]{2,1,0:T(8,128)}), f32[128,48,128]{2,1,0:T(8,128)}, u32[]{:S(2)}, u32[]{:S(2)}) %all-to-all-start.1) | async-done | bytes 3145760 | tf_op jit(solution)/shard_map/all_to_all | solution.py:145
  208.9 10.1 %add_rows.5.refs_1_ = f32[512,8,128]{2,1,0:T(8,128)S(1)} custom-call(s32[3072]{0:T(1024)S(1)} %reshape.27.refs_0_, f32[8,16,48,128]{3,2,1,0:T(8,128)} %bitcast.2.refs_1_, f32[512,8,128]{2,1,0:T(8,128)S(1)} %add_rows.4.refs_2_), custom_call_target="tpu_custom_call" | custom-call | tf_op jit(solution)/shard_map/add_rows/pallas_call | solution.py:78
  219.1 2.2 transform.1
  221.3 20.7 %all_to_all.26 = f32[16,4,32,128]{3,2,1,0:T(8,128)S(1)} all-to-all(f32[16,4,32,128]{3,2,1,0:T(8,128)S(1)} %transform.1), channel_id=1, replica_groups=mesh['tau'=8,'tile'=16] {'tile'}, dimensions={0} | all-to-all | bytes 2097152 | tf_op jit(solution)/shard_map/all_to_all | solution.py:152
  242.0 1.6 copy.10
  (1 shorter events, 0.0 us)
Async XLA Ops:
  1.3 15.8 %all-to-all-start = ((s32[16,1,192]{2,1,0:T(1,128)}), s32[16,1,192]{2,1,0:T(1,128)S(1)}, u32[]{:S(2)}, u32[]{:S(2)}) async-start(s32[16,1,192]{2,1,0:T(1,128)} %broadcast_in_dim.3), calls=%async_computation | async-start | bytes 32768 | tf_op jit(solution)/shard_map/all_to_all | solution.py:139
  29.4 1.6 copy-start.2
  31.0 46.6 %all-to-all-start.3 = ((f32[128,48,128]{2,1,0:T(8,128)}), f32[128,48,128]{2,1,0:T(8,128)S(1)}, u32[]{:S(2)}, u32[]{:S(2)}) async-start(f32[128,48,128]{2,1,0:T(8,128)} %copy-done.2), calls=%async_computation.3 | async-start | bytes 6291456 | tf_op jit(solution)/shard_map/all_to_all | solution.py:145
  37.3 2.2 copy-start
  77.7 85.5 %all-to-all-start.2 = ((f32[128,96,128]{2,1,0:T(8,128)}), f32[128,96,128]{2,1,0:T(8,128)}, u32[]{:S(2)}, u32[]{:S(2)}) async-start(f32[128,96,128]{2,1,0:T(8,128)} %products.4), calls=%async_computation.2 | async-start | bytes 12582912 | tf_op jit(solution)/shard_map/all_to_all | solution.py:145
  95.7 1.6 copy-start.1
  97.3 71.5 %copy-start.3 = (f32[4,8]{1,0:T(4,128)S(1)}, f32[4,8]{1,0:T(4,128)}, u32[]{:S(2)}) copy-start(f32[4,8]{1,0:T(4,128)} %param.8) | copy-start | bytes 388
  163.1 45.8 %all-to-all-start.1 = ((f32[128,48,128]{2,1,0:T(8,128)}), f32[128,48,128]{2,1,0:T(8,128)}, u32[]{:S(2)}, u32[]{:S(2)}) async-start(f32[128,48,128]{2,1,0:T(8,128)} %copy-done.1), calls=%async_computation.1 | async-start | bytes 6291456 | tf_op jit(solution)/shard_map/all_to_all | solution.py:145
